TPU v7x, 32 devices: a whole 2x2x4 slice. The times are simulated.
32 devices in a mesh: ctx: 8 (over z, x), heads: 4 (over y, core).
Axes of the slice: x: 2, y: 2, z: 4, core: 2. Of those that a mesh axis runs over, the one named last changes fastest.
Arguments:
- query_rows: bfloat16 [8, 16, 2, 128], P('ctx', 'heads'), may hold values from -6 to 6
- past_keys: bfloat16 [8, 16, 512, 128], P(None, 'heads', 'ctx'), may hold values from -6 to 6
- past_values: bfloat16 [8, 16, 512, 128], P(None, 'heads', 'ctx'), may hold values from -6 to 6
- used_length: int32 [8], replicated, may hold values from 256 to 512
Outputs:
- read: bfloat16 [8, 16, 2, 128], P('ctx', 'heads')
All inputs are finite; a program needn't handle non-finite values.
Results may differ from a plain program's by a relative error of at most 0.0015.
Values may be sent and summed in bfloat16 or wider, within the bound.
A program may use at most 64 MiB of HBM per device.

v0:
```python
import jax
import jax.numpy as jnp
from jax import lax
from jax.sharding import PartitionSpec as P

HEAD_SIZE = 128


def local(query_rows, past_keys, past_values, used_length):
    all_queries = lax.all_gather(query_rows, "ctx", axis=0, tiled=True)
    logit = jnp.einsum(
        "bkgd,bktd->bkgt", all_queries, past_keys, preferred_element_type=jnp.float32
    ) * HEAD_SIZE ** (-0.5)
    positions = lax.axis_index("ctx") * past_keys.shape[2] + jnp.arange(past_keys.shape[2])
    filled = positions[None, :] < used_length[:, None]
    logit = jnp.where(filled[:, None, None, :], logit, -1e30)
    top = jnp.max(logit, axis=-1)
    part = jnp.where(filled[:, None, None, :], jnp.exp(logit - top[..., None]), 0.0)
    weight_sum = jnp.sum(part, axis=-1)
    read_sum = jnp.einsum(
        "bkgt,bktd->bkgd", part, past_values.astype(jnp.float32), precision=lax.Precision.HIGHEST
    )
    tops, sums, parts = (
        lax.all_to_all(top[None], "ctx", split_axis=1, concat_axis=0, tiled=True),
        lax.all_to_all(weight_sum[None], "ctx", split_axis=1, concat_axis=0, tiled=True),
        lax.all_to_all(read_sum[None], "ctx", split_axis=1, concat_axis=0, tiled=True),
    )
    best = jnp.max(tops, axis=0)
    scale = jnp.exp(tops - best)
    weight_own = jnp.sum(sums * scale, axis=0)
    read_own = jnp.sum(parts * scale[..., None], axis=0)
    read = (read_own / weight_own[..., None]).astype(jnp.bfloat16)
    return read


def solution(mesh):
    return jax.shard_map(
        local,
        mesh=mesh,
        in_specs=(
            P("ctx", "heads", None, None),
            P(None, "heads", "ctx", None),
            P(None, "heads", "ctx", None),
            P(),
        ),
        out_specs=P("ctx", "heads", None, None),
        check_vma=False,
    )
```

profile of v0, /device:TPU:0, one launch (start us, length us, event | category | flops | bytes accessed | tf_op | source)
XLA Modules:
  0.0 68.0 jit_solution(10074065572557208397)
XLA Ops:
  0.0 0.0 copy-start
  0.0 0.0 copy-start.1
  0.0 0.7 %copy-done.1 = bf16[1,4,2,128]{3,2,1,0:T(2,128)(2,1)S(1)} copy-done((bf16[1,4,2,128]{3,2,1,0:T(2,128)(2,1)S(1)}, bf16[1,4,2,128]{3,2,1,0:T(2,128)(2,1)}, u32[]{:S(2)}) %copy-start.1) | copy-done | bytes 2072
  0.7 0.0 copy-start.2
  0.8 32.4 %all_gather.3 = bf16[8,4,2,128]{3,1,2,0:T(4,128)(2,1)S(1)} all-gather(bf16[1,4,2,128]{3,1,2,0:T(4,128)(2,1)S(1)} %copy.7), channel_id=1, replica_groups=mesh['ctx'=8,'heads'=4] {'ctx'}, dimensions={0}, use_global_device_ids=true | all-gather | bytes 18432 | tf_op jit(solution)/shard_map/all_gather | solution.py:10
  33.2 0.0 copy-done.2
  33.2 0.1 broadcast_compare_fusion
  33.2 1.5 %fusion.10 = (f32[8,4,2]{2,1,0:T(4,128)S(1)}, f32[8,4,2,64]{3,2,1,0:T(2,128)S(1)}) fusion(bf16[8,4,64,128]{3,2,1,0:T(8,128)(2,1)} %param.5, bf16[8,4,2,128]{3,1,2,0:T(4,128)(2,1)S(1)} %all_gather.3, pred[8,64]{1,0:T(8,128)(4,1)S(1)} %broadcast_compare_fusion), kind=kOutput, calls=%fused_computation.19 | convolution fusion | flops 1060800 | bytes 557824 | tf_op jit(solution)/shard_map/bkgd,bktd->bkgt/dot_general | solution.py:11
  34.7 0.7 %copy.11 = f32[1,8,4,2]{2,3,0,1:T(2,128)} copy(f32[1,8,4,2]{3,2,1,0:T(4,128)S(1)} %bitcast.30) | data formatting | bytes 512 | tf_op jit(solution)/shard_map/broadcast_in_dim | solution.py:24
  35.5 5.5 %all-to-all-start.1 = ((f32[1,8,4,2]{2,3,0,1:T(2,128)}), f32[1,8,4,2]{2,3,0,1:T(2,128)S(1)}, u32[]{:S(2)}, u32[]{:S(2)}) async-start(f32[1,8,4,2]{2,3,0,1:T(2,128)} %copy.11), calls=%async_computation.1 | async-start | bytes 16384 | tf_op jit(solution)/shard_map/all_to_all | solution.py:24
  40.9 0.0 copy-done
  40.9 1.2 %convolution_bitcast_fusion = f32[1,8,4,2,128]{4,3,2,0,1:T(2,128)} fusion(bf16[8,4,64,128]{3,2,1,0:T(8,128)(2,1)S(1)} %copy-done, f32[8,4,2,64]{3,2,1,0:T(2,128)S(1)} %get-tuple-element.6, pred[8,64]{1,0:T(8,128)(4,1)S(1)} %broadcast_compare_fusion, f32[8,4,2]{2,1,0:T(4,128)S(1)} %get-tuple-element.5), kind=kOutput, calls=%fused_computation | convolution fusion | flops 6299648 | bytes 574208 | tf_op jit(solution)/shard_map/bkgt,bktd->bkgd/dot_general | solution.py:20
  42.1 0.2 fusion.8
  42.4 0.7 %copy.15 = f32[1,8,4,2]{2,3,0,1:T(2,128)} copy(f32[1,8,4,2]{3,2,1,0:T(4,128)S(1)} %bitcast.31) | data formatting | bytes 512 | tf_op jit(solution)/shard_map/broadcast_in_dim | solution.py:25
  43.1 4.4 %all-to-all-done.1 = f32[1,8,4,2]{2,3,0,1:T(2,128)S(1)} async-done(((f32[1,8,4,2]{2,3,0,1:T(2,128)}), f32[1,8,4,2]{2,3,0,1:T(2,128)S(1)}, u32[]{:S(2)}, u32[]{:S(2)}) %all-to-all-start.1) | async-done | bytes 288 | tf_op jit(solution)/shard_map/all_to_all | solution.py:24
  47.5 3.3 %all-to-all-start.2 = ((f32[1,8,4,2]{2,3,0,1:T(2,128)}), f32[1,8,4,2]{2,3,0,1:T(2,128)S(1)}, u32[]{:S(2)}, u32[]{:S(2)}) async-start(f32[1,8,4,2]{2,3,0,1:T(2,128)} %copy.15), calls=%async_computation.2 | async-start | bytes 16384 | tf_op jit(solution)/shard_map/all_to_all | solution.py:25
  50.8 0.1 copy.12
  50.9 0.1 fusion.6
  51.0 6.3 %all-to-all-done.2 = f32[1,8,4,2]{2,3,0,1:T(2,128)S(1)} async-done(((f32[1,8,4,2]{2,3,0,1:T(2,128)}), f32[1,8,4,2]{2,3,0,1:T(2,128)S(1)}, u32[]{:S(2)}, u32[]{:S(2)}) %all-to-all-start.2) | async-done | bytes 288 | tf_op jit(solution)/shard_map/all_to_all | solution.py:25
  57.3 3.3 %all-to-all-start = ((f32[1,8,4,2,128]{4,3,2,0,1:T(2,128)}), f32[1,8,4,2,128]{4,3,2,0,1:T(2,128)S(1)}, u32[]{:S(2)}, u32[]{:S(2)}) async-start(f32[1,8,4,2,128]{4,3,2,0,1:T(2,128)} %convolution_bitcast_fusion), calls=%async_computation | async-start | bytes 65536 | tf_op jit(solution)/shard_map/all_to_all | solution.py:26
  60.6 0.1 copy.16
  60.7 0.2 fusion.5
  60.9 0.1 copy.18
  61.0 0.1 copy.13
  61.1 6.2 %all-to-all-done = f32[1,8,4,2,128]{4,3,2,0,1:T(2,128)S(1)} async-done(((f32[1,8,4,2,128]{4,3,2,0,1:T(2,128)}), f32[1,8,4,2,128]{4,3,2,0,1:T(2,128)S(1)}, u32[]{:S(2)}, u32[]{:S(2)}) %all-to-all-start) | async-done | bytes 32800 | tf_op jit(solution)/shard_map/all_to_all | solution.py:26
  67.2 0.1 fusion.1
  67.4 0.7 fusion.7
  (3 shorter events, 0.0 us)
Async XLA Ops:
  0.0 40.9 %copy-start = (bf16[8,4,64,128]{3,2,1,0:T(8,128)(2,1)S(1)}, bf16[8,4,64,128]{3,2,1,0:T(8,128)(2,1)}, u32[]{:S(2)}) copy-start(bf16[8,4,64,128]{3,2,1,0:T(8,128)(2,1)} %param.6) | copy-start | bytes 1572868
  0.0 0.7 %copy-start.1 = (bf16[1,4,2,128]{3,2,1,0:T(2,128)(2,1)S(1)}, bf16[1,4,2,128]{3,2,1,0:T(2,128)(2,1)}, u32[]{:S(2)}) copy-start(bf16[1,4,2,128]{3,2,1,0:T(2,128)(2,1)} %param.4) | copy-start | bytes 6148
  0.7 32.4 %copy-start.2 = (s32[8]{0:T(128)S(1)}, s32[8]{0:T(128)}, u32[]{:S(2)}) copy-start(s32[8]{0:T(128)} %param.7) | copy-start | bytes 100
  35.5 12.0 %all-to-all-start.1 = ((f32[1,8,4,2]{2,3,0,1:T(2,128)}), f32[1,8,4,2]{2,3,0,1:T(2,128)S(1)}, u32[]{:S(2)}, u32[]{:S(2)}) async-start(f32[1,8,4,2]{2,3,0,1:T(2,128)} %copy.11), calls=%async_computation.1 | async-start | bytes 16384 | tf_op jit(solution)/shard_map/all_to_all | solution.py:24
  47.5 9.8 %all-to-all-start.2 = ((f32[1,8,4,2]{2,3,0,1:T(2,128)}), f32[1,8,4,2]{2,3,0,1:T(2,128)S(1)}, u32[]{:S(2)}, u32[]{:S(2)}) async-start(f32[1,8,4,2]{2,3,0,1:T(2,128)} %copy.15), calls=%async_computation.2 | async-start | bytes 16384 | tf_op jit(solution)/shard_map/all_to_all | solution.py:25
  57.3 10.0 %all-to-all-start = ((f32[1,8,4,2,128]{4,3,2,0,1:T(2,128)}), f32[1,8,4,2,128]{4,3,2,0,1:T(2,128)S(1)}, u32[]{:S(2)}, u32[]{:S(2)}) async-start(f32[1,8,4,2,128]{4,3,2,0,1:T(2,128)} %convolution_bitcast_fusion), calls=%async_computation | async-start | bytes 65536 | tf_op jit(solution)/shard_map/all_to_all | solution.py:26
where the time goes:
time: 68.4 us; the launch traced here: 68 us
  blocking collectives  32.4 us (47%)
  waiting for transfers between devices  16.8 us (25%)
  starting transfers between devices  12.1 us (18%)
  matrix products  2.71 us (4%)
  local copies, waits for them, and re-layouts  2.59 us (4%)
  other arithmetic  1.32 us (2%)
    all_gather x1, blocking collectives, local(): all_queries = lax.all_gather(query_rows, 'ctx', axis=0, tiled=True)  32.4 us
    all_to_all x1, waiting for transfers between devices, local(): lax.all_to_all(weight_sum[None], 'ctx', split_axis=1, concat_axis=0, tile...  6.29 us
    all_to_all x1, waiting for transfers between devices, local(): lax.all_to_all(read_sum[None], 'ctx', split_axis=1, concat_axis=0, tiled=...  6.17 us
    all_to_all x1, starting transfers between devices, local(): lax.all_to_all(top[None], 'ctx', split_axis=1, concat_axis=0, tiled=True)  5.46 us
    all_to_all x1, waiting for transfers between devices, local(): lax.all_to_all(top[None], 'ctx', split_axis=1, concat_axis=0, tiled=True)  4.38 us
    all_to_all x1, starting transfers between devices, local(): lax.all_to_all(read_sum[None], 'ctx', split_axis=1, concat_axis=0, tiled=...  3.33 us
    all_to_all x1, starting transfers between devices, local(): lax.all_to_all(weight_sum[None], 'ctx', split_axis=1, concat_axis=0, tile...  3.32 us
    dot_general x1, matrix products, local(): jnp.einsum('bkgd,bktd->bkgt', all_queries, past_keys, preferred_element_t...  1.51 us
  transfers between devices with their start and end apart: 3, of which 3 were waited for; matrix products, arithmetic and copies ran while one was open for 4% of the time, Pallas kernels for 0%

commit v1 on v0

v1 whole, which is shorter than its diff:
```python
import functools

import jax
import jax.numpy as jnp
from jax import lax
from jax.experimental import pallas as pl
from jax.experimental.pallas import tpu as pltpu
from jax.sharding import PartitionSpec as P

MESH = pl.DeviceIdType.MESH


def partner(me, step, n):
    if n & (n - 1):
        return lax.rem(me + step, n), lax.rem(me + n - step, n)
    peer, bit = 0, 1
    while bit < n:
        own = lax.rem(me // bit, 2)
        peer = peer + bit * (1 - own if step & bit else own)
        bit *= 2
    return peer, peer


def groups_of(n):
    groups, start = [[0]], 1
    while start < n:
        groups.append(list(range(start, min(2 * start + 2, n))))
        start = groups[-1][-1] + 1
    return groups


def kernel(
    n, per, heads, group, scale,
    q_hbm, k_hbm, v_hbm, length_hbm, out_ref,
    queries, keys, values, length, sent, landed,
    local_sem, q_send, q_recv, part_send, part_recv,
):
    me = lax.axis_index("ctx")
    rows = heads * group
    width = keys.shape[1]
    stretch = width // heads
    to = [partner(me, s, n)[0] for s in range(n)]
    source = [partner(me, s, n)[1] for s in range(n)]

    local = [
        pltpu.make_async_copy(q_hbm, queries.at[0], local_sem.at[0]),
        pltpu.make_async_copy(length_hbm, length, local_sem.at[1]),
        pltpu.make_async_copy(k_hbm, keys, local_sem.at[2]),
        pltpu.make_async_copy(v_hbm, values, local_sem.at[3]),
    ]
    barrier = pltpu.get_barrier_semaphore()
    for s in range(n - 1, 0, -1):
        pl.semaphore_signal(barrier, inc=1, device_id={"ctx": to[s]}, device_id_type=MESH)
    for copy in local:
        copy.start()
    local[0].wait()
    pl.semaphore_wait(barrier, n - 1)

    asked = {}
    for s in range(n - 1, 0, -1):
        asked[s] = pltpu.make_async_remote_copy(
            src_ref=queries.at[0], dst_ref=queries.at[s],
            send_sem=q_send.at[s], recv_sem=q_recv.at[s],
            device_id={"ctx": to[s]}, device_id_type=MESH,
        )
        asked[s].start()
    for copy in local[1:]:
        copy.wait()

    row = lax.broadcasted_iota(jnp.int32, (rows, width), 0)
    column = lax.broadcasted_iota(jnp.int32, (rows, width), 1)
    same_head = (row // group) == (column // stretch)
    position = me * stretch + lax.rem(column, stretch)
    left = lax.broadcasted_iota(jnp.int32, (rows, 128), 1) < 64
    answers = {}
    for steps in groups_of(n):
        for s in steps:
            if s:
                asked[s].wait_recv()
        for s in steps:
            for j in range(per):
                b = source[s] * per + j
                logit = lax.dot_general(
                    queries[s, j], keys[b], (((1,), (1,)), ((), ())),
                    preferred_element_type=jnp.float32,
                ) * scale
                filled = same_head & (position < length[b])
                logit = jnp.where(filled, logit, -1e30)
                top = jnp.max(logit, axis=-1, keepdims=True)
                part = jnp.where(filled, jnp.exp(logit - top), 0.0)
                weight = jnp.sum(part, axis=-1, keepdims=True)
                high = part.astype(jnp.bfloat16)
                low = (part - high.astype(jnp.float32)).astype(jnp.bfloat16)
                both = jnp.dot(
                    jnp.concatenate([high, low], axis=0), values[b],
                    preferred_element_type=jnp.float32,
                )
                slot = sent if s else landed
                slot[s, j, :rows] = both[:rows] + both[rows:]
                slot[s, j, rows:] = jnp.where(left, top, weight)
        for s in steps:
            if s:
                answers[s] = pltpu.make_async_remote_copy(
                    src_ref=sent.at[s], dst_ref=landed.at[s],
                    send_sem=part_send.at[s], recv_sem=part_recv.at[s],
                    device_id={"ctx": source[s]}, device_id_type=MESH,
                )
                answers[s].start()
    for s in range(1, n):
        answers[s].wait_recv()
    for j in range(per):
        tops = [landed[s, j, rows:, 0:1] for s in range(n)]
        weights = [landed[s, j, rows:, 64:65] for s in range(n)]
        best = functools.reduce(jnp.maximum, tops)
        scales = [jnp.exp(top - best) for top in tops]
        total = sum(weight * by for weight, by in zip(weights, scales))
        read = sum(landed[s, j, :rows] * scales[s] for s in range(n))
        out_ref[j * rows:(j + 1) * rows] = (read / total).astype(out_ref.dtype)
    for s in range(1, n):
        asked[s].wait_send()
        answers[s].wait_send()


def solution(mesh):
    n = mesh.shape["ctx"]

    def local(query_rows, past_keys, past_values, used_length):
        per, heads, group, size = query_rows.shape
        batch, _, stretch, _ = past_keys.shape
        rows, width = heads * group, heads * stretch
        any_space = pl.BlockSpec(memory_space=pl.ANY)
        out = pl.pallas_call(
            functools.partial(kernel, n, per, heads, group, size ** -0.5),
            out_shape=jax.ShapeDtypeStruct((per * rows, size), query_rows.dtype),
            in_specs=[any_space] * 4,
            out_specs=pl.BlockSpec(memory_space=pltpu.VMEM),
            scratch_shapes=[
                pltpu.VMEM((n, per, rows, size), query_rows.dtype),
                pltpu.VMEM((batch, width, size), past_keys.dtype),
                pltpu.VMEM((batch, width, size), past_values.dtype),
                pltpu.SMEM((batch,), jnp.int32),
                pltpu.VMEM((n, per, 2 * rows, size), jnp.float32),
                pltpu.VMEM((n, per, 2 * rows, size), jnp.float32),
                pltpu.SemaphoreType.DMA((4,)),
                pltpu.SemaphoreType.DMA((n,)),
                pltpu.SemaphoreType.DMA((n,)),
                pltpu.SemaphoreType.DMA((n,)),
                pltpu.SemaphoreType.DMA((n,)),
            ],
            compiler_params=pltpu.CompilerParams(collective_id=0, has_side_effects=True),
        )(
            query_rows.reshape(per, rows, size),
            past_keys.reshape(batch, width, size),
            past_values.reshape(batch, width, size),
            used_length,
        )
        return out.reshape(query_rows.shape)

    return jax.shard_map(
        local,
        mesh=mesh,
        in_specs=(
            P("ctx", "heads", None, None),
            P(None, "heads", "ctx", None),
            P(None, "heads", "ctx", None),
            P(),
        ),
        out_specs=P("ctx", "heads", None, None),
        check_vma=False,
    )
```

time: 68.4 us -> 17.8 us (0.26)
  blocking collectives: 32.4 us -> 0 us
  waiting for transfers between devices: 16.8 us -> 0 us
  Pallas kernels: 0 us -> 16.4 us
  starting transfers between devices: 12.1 us -> 0 us
  matrix products: 2.71 us -> 0 us
  local copies, waits for them, and re-layouts: 2.59 us -> 1.26 us
  other arithmetic: 1.32 us -> 0 us
    all_gather x1 -> x0, blocking collectives: 32.4 us -> none  [local(): all_queries = lax.all_gather(query_rows, 'ctx', axis=0, tiled=True)]
    all_to_all x3 -> x0, waiting for transfers between devices: 16.8 us -> none  [the longest x1 6.29 us: local(): lax.all_to_all(weight_sum[None], 'ctx', split_axis=1, concat_axis=0, tile...]
    pallas_call x0 -> x1, Pallas kernels: none -> 16.4 us  [local(): pl.pallas_call(functools.partial(kernel, n, per, heads, group, size ** (-...]
    all_to_all x3 -> x0, starting transfers between devices: 12.1 us -> none  [the longest x1 5.46 us: local(): lax.all_to_all(top[None], 'ctx', split_axis=1, concat_axis=0, tiled=True)]
    dot_general x2 -> x0, matrix products: 2.71 us -> none  [the longest x1 1.51 us: local(): jnp.einsum('bkgd,bktd->bkgt', all_queries, past_keys, preferred_element_t...]
    broadcast_in_dim x2 -> x0, local copies, waits for them, and re-layouts: 1.46 us -> none  [the longest x1 0.73 us: local(): weight_sum[None]]
  transfers between devices with their start and end apart: 3 -> 0, of which waited for: 3 -> 0; matrix products, arithmetic and copies ran while one was open for 4% -> 0% of each run, Pallas kernels for 0% -> 0%
where the time goes in v1:
time: 17.8 us; the launch traced here: 17.7 us
  Pallas kernels  16.4 us (92%)
  local copies, waits for them, and re-layouts  1.26 us (7%)
    pallas_call x1, Pallas kernels, local(): pl.pallas_call(functools.partial(kernel, n, per, heads, group, size ** (-...  16.4 us
    unnamed x1, local copies, waits for them, and re-layouts  1.26 us

profile of v1, /device:TPU:0, one launch (start us, length us, event | category | flops | bytes accessed | tf_op | source)
XLA Modules:
  0.0 17.7 jit_solution(374202917473251401)
XLA Ops:
  0.0 16.4 %shard_map.46 = bf16[8,128]{1,0:T(8,128)(2,1)} custom-call(bf16[1,8,128]{2,1,0:T(8,128)(2,1)} %bitcast.7, bf16[8,256,128]{2,1,0:T(8,128)(2,1)} %bitcast.4, bf16[8,256,128]{2,1,0:T(8,128)(2,1)} %bitcast.5, s32[8]{0:T(128)} %length_hbm.1), custom_call_target="tpu_custom_call" | custom-call | tf_op jit(solution)/shard_map/pallas_call | solution.py:132
  16.4 1.3 %copy.6 = bf16[1,4,2,128]{3,2,1,0:T(2,128)(2,1)} copy(bf16[1,4,2,128]{3,2,1,0:T(2,128)(2,1)} %bitcast.6) | data formatting | bytes 4096

commit v2 on v1

--- a/solution.py
+++ b/solution.py
@@ -22,11 +22,7 @@
 
 
 def groups_of(n):
-    groups, start = [[0]], 1
-    while start < n:
-        groups.append(list(range(start, min(2 * start + 2, n))))
-        start = groups[-1][-1] + 1
-    return groups
+    return [[s] for s in range(n)]
 
 
 def kernel(
@@ -131,7 +127,7 @@
         any_space = pl.BlockSpec(memory_space=pl.ANY)
         out = pl.pallas_call(
             functools.partial(kernel, n, per, heads, group, size ** -0.5),
-            out_shape=jax.ShapeDtypeStruct((per * rows, size), query_rows.dtype),
+            out_shape=pltpu.VMEM((per * rows, size), query_rows.dtype),
             in_specs=[any_space] * 4,
             out_specs=pl.BlockSpec(memory_space=pltpu.VMEM),
             scratch_shapes=[

time: 17.8 us -> 15.6 us (0.88)
  Pallas kernels: 16.4 us -> 14.8 us
  local copies, waits for them, and re-layouts: 1.26 us -> 0.58 us
    pallas_call x1, Pallas kernels: 16.4 us -> 14.8 us  [local(): pl.pallas_call(functools.partial(kernel, n, per, heads, group, size ** (-...]
    unnamed x1, local copies, waits for them, and re-layouts: 1.26 us -> 0.58 us
where the time goes in v2:
time: 15.6 us; the launch traced here: 15.4 us
  Pallas kernels  14.8 us (95%)
  local copies, waits for them, and re-layouts  0.58 us (4%)
    pallas_call x1, Pallas kernels, local(): pl.pallas_call(functools.partial(kernel, n, per, heads, group, size ** (-...  14.8 us
    unnamed x1, local copies, waits for them, and re-layouts  0.58 us

profile of v2, /device:TPU:0, one launch (start us, length us, event | category | flops | bytes accessed | tf_op | source)
XLA Modules:
  0.0 15.4 jit_solution(15549027384302908853)
XLA Ops:
  0.0 14.8 %shard_map.46 = bf16[8,128]{1,0:T(8,128)(2,1)S(1)} custom-call(bf16[1,8,128]{2,1,0:T(8,128)(2,1)} %bitcast.7, bf16[8,256,128]{2,1,0:T(8,128)(2,1)} %bitcast.5, bf16[8,256,128]{2,1,0:T(8,128)(2,1)} %bitcast.6, s32[8]{0:T(128)} %length_hbm.1), custom_call_target="tpu_custom_call" | custom-call | tf_op jit(solution)/shard_map/pallas_call | solution.py:128
  14.8 0.6 %copy.6 = bf16[1,4,2,128]{3,2,1,0:T(2,128)(2,1)} copy(bf16[1,4,2,128]{3,2,1,0:T(2,128)(2,1)S(1)} %bitcast.4) | data formatting | bytes 4096

commit v3 on v2

--- a/solution.py
+++ b/solution.py
@@ -21,8 +21,13 @@
     return peer, peer
 
 
-def groups_of(n):
-    return [[s] for s in range(n)]
+def reach(n):
+    if n & (n - 1):
+        return n
+    near = 1
+    while near * near < n:
+        near *= 2
+    return near
 
 
 def kernel(
@@ -45,21 +50,28 @@
         pltpu.make_async_copy(v_hbm, values, local_sem.at[3]),
     ]
     barrier = pltpu.get_barrier_semaphore()
-    for s in range(n - 1, 0, -1):
+    near = reach(n)
+    far = list(range(near, n, near))
+    direct = far + list(range(near - 1, 0, -1))
+    for s in direct:
         pl.semaphore_signal(barrier, inc=1, device_id={"ctx": to[s]}, device_id_type=MESH)
     for copy in local:
         copy.start()
     local[0].wait()
-    pl.semaphore_wait(barrier, n - 1)
+    pl.semaphore_wait(barrier, len(direct))
 
     asked = {}
-    for s in range(n - 1, 0, -1):
-        asked[s] = pltpu.make_async_remote_copy(
-            src_ref=queries.at[0], dst_ref=queries.at[s],
-            send_sem=q_send.at[s], recv_sem=q_recv.at[s],
-            device_id={"ctx": to[s]}, device_id_type=MESH,
+
+    def ask(slot, target, origin):
+        asked[slot] = pltpu.make_async_remote_copy(
+            src_ref=queries.at[origin], dst_ref=queries.at[slot],
+            send_sem=q_send.at[slot], recv_sem=q_recv.at[slot],
+            device_id={"ctx": to[target]}, device_id_type=MESH,
         )
-        asked[s].start()
+        asked[slot].start()
+
+    for s in direct:
+        ask(s, s, 0)
     for copy in local[1:]:
         copy.wait()
 
@@ -69,39 +81,49 @@
     position = me * stretch + lax.rem(column, stretch)
     left = lax.broadcasted_iota(jnp.int32, (rows, 128), 1) < 64
     answers = {}
-    for steps in groups_of(n):
-        for s in steps:
-            if s:
-                asked[s].wait_recv()
-        for s in steps:
-            for j in range(per):
-                b = source[s] * per + j
-                logit = lax.dot_general(
-                    queries[s, j], keys[b], (((1,), (1,)), ((), ())),
-                    preferred_element_type=jnp.float32,
-                ) * scale
-                filled = same_head & (position < length[b])
-                logit = jnp.where(filled, logit, -1e30)
-                top = jnp.max(logit, axis=-1, keepdims=True)
-                part = jnp.where(filled, jnp.exp(logit - top), 0.0)
-                weight = jnp.sum(part, axis=-1, keepdims=True)
-                high = part.astype(jnp.bfloat16)
-                low = (part - high.astype(jnp.float32)).astype(jnp.bfloat16)
-                both = jnp.dot(
-                    jnp.concatenate([high, low], axis=0), values[b],
-                    preferred_element_type=jnp.float32,
-                )
-                slot = sent if s else landed
-                slot[s, j, :rows] = both[:rows] + both[rows:]
-                slot[s, j, rows:] = jnp.where(left, top, weight)
-        for s in steps:
-            if s:
-                answers[s] = pltpu.make_async_remote_copy(
-                    src_ref=sent.at[s], dst_ref=landed.at[s],
-                    send_sem=part_send.at[s], recv_sem=part_recv.at[s],
-                    device_id={"ctx": source[s]}, device_id_type=MESH,
-                )
-                answers[s].start()
+
+    def answer(s):
+        for j in range(per):
+            b = source[s] * per + j
+            logit = lax.dot_general(
+                queries[s, j], keys[b], (((1,), (1,)), ((), ())),
+                preferred_element_type=jnp.float32,
+            ) * scale
+            filled = same_head & (position < length[b])
+            logit = jnp.where(filled, logit, -1e30)
+            top = jnp.max(logit, axis=-1, keepdims=True)
+            part = jnp.where(filled, jnp.exp(logit - top), 0.0)
+            weight = jnp.sum(part, axis=-1, keepdims=True)
+            high = part.astype(jnp.bfloat16)
+            low = (part - high.astype(jnp.float32)).astype(jnp.bfloat16)
+            both = jnp.dot(
+                jnp.concatenate([high, low], axis=0), values[b],
+                preferred_element_type=jnp.float32,
+            )
+            slot = sent if s else landed
+            slot[s, j, :rows] = both[:rows] + both[rows:]
+            slot[s, j, rows:] = jnp.where(left, top, weight)
+        if s:
+            answers[s] = pltpu.make_async_remote_copy(
+                src_ref=sent.at[s], dst_ref=landed.at[s],
+                send_sem=part_send.at[s], recv_sem=part_recv.at[s],
+                device_id={"ctx": source[s]}, device_id_type=MESH,
+            )
+            answers[s].start()
+
+    answer(0)
+    for high in far:
+        asked[high].wait_recv()
+        for low in range(near - 1, 0, -1):
+            ask(high + low, low, high)
+    for s in range(1, near):
+        asked[s].wait_recv()
+        answer(s)
+    for high in far:
+        answer(high)
+        for low in range(1, near):
+            asked[high + low].wait_recv()
+            answer(high + low)
     for s in range(1, n):
         answers[s].wait_recv()
     for j in range(per):

time: 15.6 us -> 16.6 us (1.064)
  Pallas kernels: 14.8 us -> 15.8 us
    pallas_call x1, Pallas kernels: 14.8 us -> 15.8 us  [local(): pl.pallas_call(functools.partial(kernel, n, per, heads, group, size ** (-...]
where the time goes in v3:
time: 16.6 us; the launch traced here: 16.4 us
  Pallas kernels  15.8 us (95%)
  local copies, waits for them, and re-layouts  0.58 us (3%)
    pallas_call x1, Pallas kernels, local(): pl.pallas_call(functools.partial(kernel, n, per, heads, group, size ** (-...  15.8 us
    unnamed x1, local copies, waits for them, and re-layouts  0.58 us

profile of v3, /device:TPU:0, one launch (start us, length us, event | category | flops | bytes accessed | tf_op | source)
XLA Modules:
  0.0 16.4 jit_solution(3507167560547230094)
XLA Ops:
  0.0 15.8 %shard_map.46 = bf16[8,128]{1,0:T(8,128)(2,1)S(1)} custom-call(bf16[1,8,128]{2,1,0:T(8,128)(2,1)} %bitcast.7, bf16[8,256,128]{2,1,0:T(8,128)(2,1)} %bitcast.5, bf16[8,256,128]{2,1,0:T(8,128)(2,1)} %bitcast.6, s32[8]{0:T(128)} %length_hbm.1), custom_call_target="tpu_custom_call" | custom-call | tf_op jit(solution)/shard_map/pallas_call | solution.py:150
  15.8 0.6 %copy.6 = bf16[1,4,2,128]{3,2,1,0:T(2,128)(2,1)} copy(bf16[1,4,2,128]{3,2,1,0:T(2,128)(2,1)S(1)} %bitcast.4) | data formatting | bytes 4096

commit v4 on v2

--- a/solution.py
+++ b/solution.py
@@ -67,7 +67,10 @@
     column = lax.broadcasted_iota(jnp.int32, (rows, width), 1)
     same_head = (row // group) == (column // stretch)
     position = me * stretch + lax.rem(column, stretch)
-    left = lax.broadcasted_iota(jnp.int32, (rows, 128), 1) < 64
+    filled = {
+        (s, j): same_head & (position < length[source[s] * per + j])
+        for s in range(n) for j in range(per)
+    }
     answers = {}
     for steps in groups_of(n):
         for s in steps:
@@ -80,11 +83,12 @@
                     queries[s, j], keys[b], (((1,), (1,)), ((), ())),
                     preferred_element_type=jnp.float32,
                 ) * scale
-                filled = same_head & (position < length[b])
-                logit = jnp.where(filled, logit, -1e30)
+                logit = jnp.where(filled[s, j], logit, -1e30)
                 top = jnp.max(logit, axis=-1, keepdims=True)
-                part = jnp.where(filled, jnp.exp(logit - top), 0.0)
-                weight = jnp.sum(part, axis=-1, keepdims=True)
+                part = jnp.where(filled[s, j], jnp.exp(logit - top), 0.0)
+                weight = jnp.maximum(jnp.sum(part, axis=-1, keepdims=True), 1.0)
+                inverse = 1.0 / weight
+                level = top + jnp.log(weight)
                 high = part.astype(jnp.bfloat16)
                 low = (part - high.astype(jnp.float32)).astype(jnp.bfloat16)
                 both = jnp.dot(
@@ -92,8 +96,8 @@
                     preferred_element_type=jnp.float32,
                 )
                 slot = sent if s else landed
-                slot[s, j, :rows] = both[:rows] + both[rows:]
-                slot[s, j, rows:] = jnp.where(left, top, weight)
+                slot[s, j, :rows] = (both[:rows] + both[rows:]) * inverse
+                slot[s, j, rows:] = jnp.broadcast_to(level, (rows, both.shape[1]))
         for s in steps:
             if s:
                 answers[s] = pltpu.make_async_remote_copy(
@@ -102,16 +106,20 @@
                     device_id={"ctx": source[s]}, device_id_type=MESH,
                 )
                 answers[s].start()
+    best = [landed[0, j, rows:] for j in range(per)]
+    read = [landed[0, j, :rows] for j in range(per)]
+    total = [jnp.ones_like(x) for x in best]
     for s in range(1, n):
         answers[s].wait_recv()
+        for j in range(per):
+            level = landed[s, j, rows:]
+            higher = jnp.maximum(best[j], level)
+            old, new = jnp.exp(best[j] - higher), jnp.exp(level - higher)
+            read[j] = read[j] * old + landed[s, j, :rows] * new
+            total[j] = total[j] * old + new
+            best[j] = higher
     for j in range(per):
-        tops = [landed[s, j, rows:, 0:1] for s in range(n)]
-        weights = [landed[s, j, rows:, 64:65] for s in range(n)]
-        best = functools.reduce(jnp.maximum, tops)
-        scales = [jnp.exp(top - best) for top in tops]
-        total = sum(weight * by for weight, by in zip(weights, scales))
-        read = sum(landed[s, j, :rows] * scales[s] for s in range(n))
-        out_ref[j * rows:(j + 1) * rows] = (read / total).astype(out_ref.dtype)
+        out_ref[j * rows:(j + 1) * rows] = (read[j] / total[j]).astype(out_ref.dtype)
     for s in range(1, n):
         asked[s].wait_send()
         answers[s].wait_send()

time: 15.6 us -> 15.4 us (0.987)
  no operation moved by 1% of the time
where the time goes in v4:
time: 15.4 us; the launch traced here: 15.3 us
  Pallas kernels  14.7 us (95%)
  local copies, waits for them, and re-layouts  0.58 us (4%)
    pallas_call x1, Pallas kernels, local(): pl.pallas_call(functools.partial(kernel, n, per, heads, group, size ** (-...  14.7 us
    unnamed x1, local copies, waits for them, and re-layouts  0.58 us

profile of v4, /device:TPU:0, one launch (start us, length us, event | category | flops | bytes accessed | tf_op | source)
XLA Modules:
  0.0 15.3 jit_solution(17513097160828441190)
XLA Ops:
  0.0 14.7 %shard_map.46 = bf16[8,128]{1,0:T(8,128)(2,1)S(1)} custom-call(bf16[1,8,128]{2,1,0:T(8,128)(2,1)} %bitcast.7, bf16[8,256,128]{2,1,0:T(8,128)(2,1)} %bitcast.5, bf16[8,256,128]{2,1,0:T(8,128)(2,1)} %bitcast.6, s32[8]{0:T(128)} %length_hbm.1), custom_call_target="tpu_custom_call" | custom-call | tf_op jit(solution)/shard_map/pallas_call | solution.py:136
  14.7 0.6 %copy.6 = bf16[1,4,2,128]{3,2,1,0:T(2,128)(2,1)} copy(bf16[1,4,2,128]{3,2,1,0:T(2,128)(2,1)S(1)} %bitcast.4) | data formatting | bytes 4096
